TPU v7x, 32 devices: a whole 2x2x4 slice. The times are simulated.
32 devices in a mesh: elem: 8 (over z, y), comp: 2 (over x), rep: 2 (over core).
Axes of the slice: x: 2, y: 2, z: 4, core: 2. Of those that a mesh axis runs over, the one named last changes fastest.
Arguments:
- velocity: float32 [3, 10, 10, 10, 2, 6144], P(None, 'comp', None, None, None, ('elem', 'rep')), may hold values from -6 to 6
- geometry: float32 [3, 3, 10, 10, 10, 2, 6144], P(None, None, 'comp', None, None, None, ('elem', 'rep')), may hold values from -40 to 40
- element_place: int32 [2, 6144], P('comp', ('elem', 'rep')), may hold values from 0 to 383, as said below
Outputs:
- pressure: float32 [10, 10, 10, 2, 6144], P(None, None, None, 'comp', ('elem', 'rep'))
Inputs may be any that keep to these rules, and one draw needn't show every extreme that they name: `element_place`: in each row and each aligned run of 384 entries of it, every value 0 to 383 appears once.
All inputs are finite; a program needn't handle non-finite values.
Results may differ from a plain program's by a relative error of at most 0.000071.
Values sent between devices are 32-bit elements; how exact they have to be, the bound alone decides.
No kernel may reach another device: no remote copies, remote signals or barrier semaphores. Data moves between devices by JAX's collectives and lax.ppermute only.
A program may use at most 192 MiB of HBM per device.

v0:
```python
import jax
import jax.numpy as jnp
import numpy as np
from jax import lax
from jax.sharding import PartitionSpec as P

BLOCK_X = 6
BLOCK_Y = 8
BLOCK_Z = 8
GRID_Y = 4
exact_mode = lax.Precision.HIGHEST


def passed_along(x, axis, by):
    count = lax.axis_size(axis)
    pairs = [(i, i + by) for i in range(count) if 0 <= i + by < count]
    return lax.ppermute(x, axis, pairs)


def legendre_columns(points, degree):
    columns = [points * 0.0 + 1.0, points]
    for order in range(2, degree + 1):
        columns.append(
            ((2 * order - 1) * points * columns[order - 1] - (order - 1) * columns[order - 2])
            / order
        )
    return columns


def derivative_table(node_count):
    degree = node_count - 1
    points = np.cos(np.pi * np.arange(node_count) / degree)
    for sweep in range(100):
        columns = legendre_columns(points, degree)
        points = points - (points * columns[degree] - columns[degree - 1]) / (
            node_count * columns[degree]
        )
    points = np.sort(points)
    values = legendre_columns(points, degree)[degree]
    identity = np.eye(node_count)
    spacing = points[:, None] - points[None, :] + identity
    matrix = values[:, None] / (values[None, :] * spacing)
    matrix = np.where(identity > 0.5, 0.0, matrix)
    matrix[0, 0] = -degree * (degree + 1) / 4.0
    matrix[degree, degree] = degree * (degree + 1) / 4.0
    return matrix


def apply_transpose(deriv_table, flux_r, flux_s, flux_t):
    along_r = jnp.einsum("ia,i...->a...", deriv_table, flux_r, precision=exact_mode)
    along_s = jnp.einsum("ib,ai...->ab...", deriv_table, flux_s, precision=exact_mode)
    along_t = jnp.einsum("ic,abi...->abc...", deriv_table, flux_t, precision=exact_mode)
    return along_r + along_s + along_t


def local_pass(field, direction, block_grid):
    last_node = field.shape[0] - 1
    element_axis = 3 + direction
    extent = block_grid[direction]
    lower = lax.slice_in_dim(field, 0, 1, axis=direction)
    upper = lax.slice_in_dim(field, last_node, last_node + 1, axis=direction)
    zero_lower = jnp.zeros_like(lax.slice_in_dim(lower, 0, 1, axis=element_axis))
    add_upper = jnp.concatenate(
        [lax.slice_in_dim(lower, 1, extent, axis=element_axis), zero_lower], axis=element_axis
    )
    add_lower = jnp.concatenate(
        [zero_lower, lax.slice_in_dim(upper, 0, extent - 1, axis=element_axis)], axis=element_axis
    )
    node_iota = lax.broadcasted_iota(jnp.int32, field.shape, direction)
    field = field + jnp.where(node_iota == 0, add_lower, 0.0)
    return field + jnp.where(node_iota == last_node, add_upper, 0.0)


def node_keep(sign_code, last_node):
    if sign_code > 0:
        return slice(last_node, last_node + 1)
    if sign_code < 0:
        return slice(0, 1)
    return slice(None)


def element_keep(sign_code, extent):
    if sign_code > 0:
        return slice(extent - 1, extent)
    if sign_code < 0:
        return slice(0, 1)
    return slice(None)


def take_region(field, offset, block_grid):
    last_node = field.shape[0] - 1
    nodes_key = tuple((node_keep(component, last_node) for component in offset))
    elems_key = tuple(
        (element_keep(offset[dim_index], block_grid[dim_index]) for dim_index in range(3))
    )
    return field[nodes_key + elems_key]


def region_mask(shape, offset, block_grid):
    last_node = shape[0] - 1
    verdict = jnp.ones(shape, dtype=jnp.bool_)
    for dim_index in range(3):
        if offset[dim_index] != 0:
            node_target = last_node if offset[dim_index] > 0 else 0
            elem_target = block_grid[dim_index] - 1 if offset[dim_index] > 0 else 0
            verdict = jnp.logical_and(
                verdict, lax.broadcasted_iota(jnp.int32, shape, dim_index) == node_target
            )
            verdict = jnp.logical_and(
                verdict, lax.broadcasted_iota(jnp.int32, shape, 3 + dim_index) == elem_target
            )
    return verdict


def add_region(field, offset, values, block_grid):
    return field + jnp.where(region_mask(field.shape, offset, block_grid), values, 0.0)


def neighbor_offsets():
    listing = []
    for step_x in (-1, 0, 1):
        for step_y in (-1, 0, 1):
            for step_z in (-1, 0, 1):
                if step_x != 0 or step_y != 0 or step_z != 0:
                    listing.append((step_x, step_y, step_z))
    return listing


def inside(position, offset, extents):
    verdict = jnp.asarray(True)
    for dim_index in range(3):
        target = position[dim_index] + offset[dim_index]
        verdict = jnp.logical_and(
            verdict, jnp.logical_and(target >= 0, target < extents[dim_index])
        )
    return verdict


def body(velocity, geometry, element_place):
    comp_count = lax.axis_size("comp")
    half_nodes = velocity.shape[1]
    node_count = half_nodes * comp_count
    deriv_table = jnp.asarray(derivative_table(node_count), jnp.float32)
    fluxes = []
    for direction in range(3):
        fluxes.append(
            geometry[0, direction] * velocity[0]
            + geometry[1, direction] * velocity[1]
            + geometry[2, direction] * velocity[2]
        )
    flux_r, flux_s, flux_t = (
        lax.all_to_all(fluxes[0], "comp", split_axis=3, concat_axis=0, tiled=True),
        lax.all_to_all(fluxes[1], "comp", split_axis=3, concat_axis=0, tiled=True),
        lax.all_to_all(fluxes[2], "comp", split_axis=3, concat_axis=0, tiled=True),
    )
    owned_nodes = apply_transpose(deriv_table, flux_r, flux_s, flux_t)
    owned_nodes = owned_nodes[:, :, :, 0, :]
    places = element_place[0]
    sub_count = places.shape[0]
    place_matrix = (places[:, None] == jnp.arange(sub_count, dtype=jnp.int32)[None, :]).astype(
        jnp.float32
    )
    canonical = jnp.einsum("abci,ij->abcj", owned_nodes, place_matrix, precision=exact_mode)
    block_grid = (BLOCK_X, BLOCK_Y, BLOCK_Z)
    canonical = canonical.reshape((node_count, node_count, node_count) + block_grid)
    layers = comp_count * lax.axis_size("rep")
    stride_x = GRID_Y * layers
    strides = (stride_x, layers, 1)
    extents = (lax.axis_size(("elem", "comp", "rep")) // stride_x, GRID_Y, layers)
    device = lax.axis_index(("elem", "comp", "rep"))
    position = (device // stride_x, device // layers % GRID_Y, device % layers)
    local_only = canonical
    for direction in range(3):
        local_only = local_pass(local_only, direction, block_grid)
    assembled = local_only
    for offset in neighbor_offsets():
        opposite = tuple((-component for component in offset))
        outgoing = take_region(local_only, opposite, block_grid)
        shift_by = -sum((component * stride for component, stride in zip(offset, strides)))
        incoming = passed_along(outgoing.reshape(-1), ("elem", "comp", "rep"), shift_by)
        within = inside(position, offset, extents)
        payload = jnp.where(within, incoming, 0.0).reshape(outgoing.shape)
        assembled = add_region(assembled, offset, payload, block_grid)
    assembled = assembled.reshape(node_count, node_count, node_count, sub_count)
    result = jnp.einsum("abcj,ij->abci", assembled, place_matrix, precision=exact_mode)
    return result[:, :, :, None, :]


def solution(mesh):
    placed = (
        P(None, "comp", None, None, None, ("elem", "rep")),
        P(None, None, "comp", None, None, None, ("elem", "rep")),
        P("comp", ("elem", "rep")),
    )
    return jax.shard_map(
        body,
        mesh=mesh,
        in_specs=placed,
        out_specs=P(None, None, None, "comp", ("elem", "rep")),
        check_vma=False,
    )
```

profile of v0, /device:TPU:7, one launch (start us, length us, event | category | flops | bytes accessed | tf_op | source)
XLA Modules:
  0.0 409.7 jit_solution(2351560866955214997)
XLA Ops:
  0.0 3.9 fusion.122
  3.9 7.8 %fusion.121 = (f32[1,1,5,10,10,2,384]{6,5,4,3,2,1,0:T(2,128)S(1)}, f32[1,1,5,10,10,2,384]{6,5,4,3,2,1,0:T(2,128)S(1)}, f32[1,1,5,10,10,2,384]{6,5,4,3,2,1,0:T(2,...) fusion(f32[3,3,5,10,10,2,384]{6,5,4,3,2,1,0:T(2,128)} %param.5), kind=kLoop, calls=%fused_computation.193 | loop fusion | bytes 27648000 | tf_op jit(solution)/shard_map/slice | solution.py:147
  11.7 4.5 %fusion.33 = (f32[5,10,10,2,384]{4,2,1,0,3:T(8,128)}, f32[5,10,10,2,384]{4,2,1,0,3:T(8,128)S(1)}, f32[5,10,10,2,384]{4,2,1,0,3:T(8,128)}) fusion(f32[1,5,10,10,2,384]{5,4,3,2,1,0:T(2,128)S(1)} %get-tuple-element.49, f32[1,1,5,10,10,2,384]{6,5,4,3,2,1,0:T(2,128)S(1)} %get-tuple-element.41, f32[1,5,10,10,2,384]{5,4,3,2,1,0:T(2,128)S(1)} %get-tuple-element.48, ...), kind=kLoop, calls=%fused_computation.61 | loop fusion | flops 5760000 | bytes 23040000 | tf_op jit(solution)/shard_map/add | solution.py:147
  16.2 30.7 %all_to_all.45 = f32[5,10,10,2,384]{4,2,1,0,3:T(8,128)} all-to-all(f32[5,10,10,2,384]{4,2,1,0,3:T(8,128)S(1)} %get-tuple-element.45), channel_id=1, replica_groups=mesh['elem'=8,'comp'=2,'rep'=2] {'comp'}, dimensions={3} | all-to-all | bytes 3072000 | tf_op jit(solution)/shard_map/all_to_all | solution.py:153
  46.9 5.1 %all-to-all-start.2 = ((f32[5,10,10,2,384]{4,2,1,0,3:T(8,128)}), f32[5,10,10,2,384]{4,2,1,0,3:T(8,128)S(1)}, u32[]{:S(2)}, u32[]{:S(2)}) async-start(f32[5,10,10,2,384]{4,2,1,0,3:T(8,128)} %get-tuple-element.46), calls=%async_computation.2 | async-start | bytes 4915200 | tf_op jit(solution)/shard_map/all_to_all | solution.py:154
  56.3 21.8 %all-to-all-done.2 = f32[5,10,10,2,384]{4,2,1,0,3:T(8,128)S(1)} async-done(((f32[5,10,10,2,384]{4,2,1,0,3:T(8,128)}), f32[5,10,10,2,384]{4,2,1,0,3:T(8,128)S(1)}, u32[]{:S(2)}, u32[]{:S(2)}) %all-to-all-start.2) | async-done | bytes 1536032 | tf_op jit(solution)/shard_map/all_to_all | solution.py:154
  78.1 6.6 %all-to-all-start = ((f32[5,10,10,2,384]{4,2,1,0,3:T(8,128)}), f32[5,10,10,2,384]{4,2,1,0,3:T(8,128)}, u32[]{:S(2)}, u32[]{:S(2)}) async-start(f32[5,10,10,2,384]{4,2,1,0,3:T(8,128)} %get-tuple-element.44), calls=%async_computation | async-start | bytes 4915200 | tf_op jit(solution)/shard_map/all_to_all | solution.py:152
  84.7 2.2 copy.25
  86.9 3.7 fusion.130
  90.7 3.7 fusion.131
  94.3 15.7 %all-to-all-done = f32[5,10,10,2,384]{4,2,1,0,3:T(8,128)} async-done(((f32[5,10,10,2,384]{4,2,1,0,3:T(8,128)}), f32[5,10,10,2,384]{4,2,1,0,3:T(8,128)}, u32[]{:S(2)}, u32[]{:S(2)}) %all-to-all-start) | async-done | bytes 1536032 | tf_op jit(solution)/shard_map/all_to_all | solution.py:152
  110.0 7.6 %fusion.37 = f32[10,10,10,384]{3,0,2,1:T(8,128)S(1)} fusion(f32[10,10,384,10]{2,3,1,0:T(8,128)} %fusion.131, f32[10,10,384,10]{2,3,1,0:T(8,128)} %fusion.130, f32[10,10,1,1]{0,1,3,2:T(8,128)S(1)} %copy-done.11, f32[10,10,10,384]{3,2,1,0:T(8,128)} %bitcast.10), kind=kOutput, calls=%fused_computation.71 | convolution fusion | flops 46848000 | bytes 6144400 | tf_op jit(solution)/shard_map/ia,i...->a.../dot_general | solution.py:50
  117.7 2.9 fusion.38
  120.6 15.3 %reshape.219 = f32[10,10,10,6,8,8]{5,4,3,2,1,0:T(8,128)} reshape(f32[10,10,10,384]{3,2,1,0:T(8,128)S(1)} %fusion.38) | data formatting | bytes 3072000 | tf_op jit(solution)/shard_map/reshape | solution.py:165
  137.3 2.9 slice.174
  140.2 1.6 slice-done.7
  141.8 2.0 fusion.129
  143.8 1.9 fusion.128
  145.7 1.5 copy-done
  147.2 20.9 %select_add_fusion.2 = f32[10,10,10,6,8,8]{5,4,3,2,1,0:T(8,128)} fusion(f32[10,10,10,6,8,8]{5,4,3,2,1,0:T(8,128)} %reshape.219, f32[10,10,6,8,8]{4,3,2,1,0:T(8,128)S(1)} %get-tuple-element.63, f32[10,10,6,8,8]{4,3,2,1,0:T(8,128)S(1)} %get-tuple-element.61, pred[10]{0:T(512)(128)(4,1)S(1)} %iota_compare_fusion.5, pred[10]{0:T(512)(128)(4,1)S(1)} %iota_compare_fusion.6), kind=kLoop, calls=%fused_computation.2 | loop fusion | flops 1536000 | bytes 3379220 | tf_op jit(solution)/shard_map/add | solution.py:71
  168.2 5.9 %fusion.120 = (f32[10,1,10,6,7,8]{5,4,3,2,1,0:T(8,128)}, f32[10,1,10,6,7,8]{5,4,3,2,1,0:T(8,128)}) fusion(f32[10,10,10,6,8,8]{5,4,3,2,1,0:T(8,128)} %select_add_fusion.2), kind=kLoop, calls=%fused_computation.192 | loop fusion | bytes 537600 | tf_op jit(solution)/shard_map/slice | solution.py:67
  174.1 6.9 %fusion.123 = (f32[10,1,10,6,8,8]{5,4,3,2,1,0:T(8,128)}, f32[10,10,6,8,8]{4,3,2,1,0:T(8,128)}, f32[10,10,6,8,8]{4,3,2,1,0:T(8,128)}, f32[10,1,10,6,8,8]{5,4,3,2,1,0:T(8,128)}) fusion(f32[10,1,10,6,7,8]{5,4,3,2,1,0:T(8,128)} %get-tuple-element.33, f32[10,1,10,6,7,8]{5,4,3,2,1,0:T(8,128)} %get-tuple-element.34), kind=kLoop, calls=%fused_computation.195 | loop fusion | bytes 883200 | tf_op jit(solution)/shard_map/concatenate | solution.py:66
  181.0 14.5 %select_add_fusion.1 = f32[10,10,10,6,8,8]{5,4,3,2,1,0:T(8,128)} fusion(f32[10,10,6,8,8]{4,3,2,1,0:T(8,128)} %get-tuple-element.64, f32[10,10,6,8,8]{4,3,2,1,0:T(8,128)} %get-tuple-element.51, pred[10]{0:T(512)(128)(4,1)S(1)} %iota_compare_fusion.5, pred[10]{0:T(512)(128)(4,1)S(1)} %iota_compare_fusion.6, f32[10,10,6,8,8]{4,3,2,1,0:T(8,128)S(1)} %get-tuple-element.63, ...), kind=kLoop, calls=%fused_computation.1 | loop fusion | flops 3072000 | bytes 3686420 | tf_op jit(solution)/shard_map/add | solution.py:71
  195.5 3.3 fusion.119
  198.8 3.0 fusion.125
  201.8 2.7 fusion.126
  204.5 17.3 %select_add_fusion = f32[10,10,10,6,8,8]{5,4,3,2,1,0:T(8,128)} fusion(f32[10,10,6,8,8]{4,3,2,1,0:T(8,128)} %get-tuple-element.57, f32[10,10,6,8,8]{4,3,2,1,0:T(8,128)} %get-tuple-element.55, pred[10]{0:T(512)(128)(4,1)S(1)} %iota_compare_fusion.5, pred[10]{0:T(512)(128)(4,1)S(1)} %iota_compare_fusion.6, f32[10,10,6,8,8]{4,3,2,1,0:T(8,128)} %get-tuple-element.64, ...), kind=kLoop, calls=%fused_computation | loop fusion | flops 4608000 | bytes 3993620 | tf_op jit(solution)/shard_map/add | solution.py:71
  221.8 1.4 fusion.117
  223.2 2.5 slice_reduce_fusion.11
  226.8 1.5 slice_reduce_fusion.15
  228.3 4.5 %slice_reduce_fusion.1 = (f32[10,10,6,8]{3,2,1,0:T(8,128)S(1)}, f32[10,10,6,8]{3,2,1,0:T(8,128)S(1)}) fusion(f32[10,10,10,6,8,8]{5,4,3,2,1,0:T(8,128)} %select_add_fusion), kind=kLoop, calls=%fused_computation.42 | loop fusion | bytes 76800 | tf_op jit(solution)/shard_map/slice | solution.py:96
  232.8 2.2 fusion.118
  235.0 5.0 %slice_reduce_fusion.3 = (f32[10,10,6,8]{3,2,1,0:T(8,128)}, f32[10,10,6,8]{3,2,1,0:T(8,128)}) fusion(f32[10,10,10,6,8,8]{5,4,3,2,1,0:T(8,128)} %select_add_fusion), kind=kLoop, calls=%fused_computation.143 | loop fusion | bytes 76800 | tf_op jit(solution)/shard_map/slice | solution.py:96
  241.3 3.6 broadcast_in_dim.442
  244.9 3.4 broadcast_in_dim.452
  248.3 1.9 broadcast_in_dim.454
  250.2 3.9 broadcast_in_dim.460
  254.2 1.9 broadcast_in_dim.462
  256.1 9.8 %collective-permute-start = (f32[1]{0:T(128)}, f32[1]{0:T(128)}, u32[]{:S(2)}, u32[]{:S(2)}) collective-permute-start(f32[1]{0:T(128)} %bitcast.39), channel_id=1, source_target_pairs={{0,21},{1,22},{2,23},{3,24},{4,25},{5,26},{6,27},{7,28},{8,29},{9,... | collective-permute-start | bytes 20 | tf_op jit(solution)/shard_map/ppermute | solution.py:17
  269.8 6.9 %collective-permute-start.8 = (f32[1]{0:T(128)}, f32[1]{0:T(128)}, u32[]{:S(2)}, u32[]{:S(2)}) collective-permute-start(f32[1]{0:T(128)} %bitcast.48), channel_id=1, source_target_pairs={{0,11},{1,12},{2,13},{3,14},{4,15},{5,16},{6,17},{7,18},{8,19},{9,... | collective-permute-start | bytes 20 | tf_op jit(solution)/shard_map/ppermute | solution.py:17
  284.8 1.8 reshape.224
  290.4 6.5 %collective-permute-start.6 = (f32[1]{0:T(128)}, f32[1]{0:T(128)}, u32[]{:S(2)}, u32[]{:S(2)}) collective-permute-start(f32[1]{0:T(128)} %bitcast.45), channel_id=1, source_target_pairs={{0,13},{1,14},{2,15},{3,16},{4,17},{5,18},{6,19},{7,20},{8,21},{9,... | collective-permute-start | bytes 20 | tf_op jit(solution)/shard_map/ppermute | solution.py:17
  297.6 2.9 collective-permute-start.2
  301.1 1.9 collective-permute-start.11
  303.7 3.6 collective-permute-start.14
  308.0 1.9 collective-permute-start.16
  310.5 4.5 %collective-permute-start.9 = (f32[60]{0:T(128)S(1)}, f32[60]{0:T(128)S(1)}, u32[]{:S(2)}, u32[]{:S(2)}) collective-permute-start(f32[60]{0:T(128)S(1)} %reshape.229), channel_id=1, source_target_pairs={{0,5},{1,6},{2,7},{3,8},{4,9},{5,10},{6,11},{7,12},{8,13},{9,14},{... | collective-permute-start | bytes 728 | tf_op jit(solution)/shard_map/ppermute | solution.py:17
  315.7 1.7 collective-permute-start.5
  320.8 7.9 %collective-permute-start.3 = (f32[80]{0:T(128)S(1)}, f32[80]{0:T(128)S(1)}, u32[]{:S(2)}, u32[]{:S(2)}) collective-permute-start(f32[80]{0:T(128)S(1)} %reshape.223), channel_id=1, source_target_pairs={{0,17},{1,18},{2,19},{3,20},{4,21},{5,22},{6,23},{7,24},{8,25},{9,... | collective-permute-start | bytes 968 | tf_op jit(solution)/shard_map/ppermute | solution.py:17
  336.5 6.7 %collective-permute-start.1 = (f32[80]{0:T(128)S(1)}, f32[80]{0:T(128)S(1)}, u32[]{:S(2)}, u32[]{:S(2)}) collective-permute-start(f32[80]{0:T(128)S(1)} %reshape.221), channel_id=1, source_target_pairs={{0,20},{1,21},{2,22},{3,23},{4,24},{5,25},{6,26},{7,27},{8,28},{9,... | collective-permute-start | bytes 968 | tf_op jit(solution)/shard_map/ppermute | solution.py:17
  343.2 1.9 collective-permute-start.13
  345.2 5.4 %collective-permute-start.12 = (f32[4800]{0:T(1024)S(1)}, f32[4800]{0:T(1024)S(1)}, u32[]{:S(2)}, u32[]{:S(2)}) collective-permute-start(f32[4800]{0:T(1024)S(1)} %reshape.232), channel_id=1, source_target_pairs={{0,1},{1,2},{2,3},{3,4},{4,5},{5,6},{6,7},{7,8},{8,9},{9,10},{10,1... | collective-permute-start | bytes 57608 | tf_op jit(solution)/shard_map/ppermute | solution.py:17
  350.6 1.9 collective-permute-start.15
  352.6 4.3 %collective-permute-start.10 = (f32[4800]{0:T(1024)S(1)}, f32[4800]{0:T(1024)S(1)}, u32[]{:S(2)}, u32[]{:S(2)}) collective-permute-start(f32[4800]{0:T(1024)S(1)} %reshape.230), channel_id=1, source_target_pairs={{0,4},{1,5},{2,6},{3,7},{4,8},{5,9},{6,10},{7,11},{8,12},{9,13},{1... | collective-permute-start | bytes 57608 | tf_op jit(solution)/shard_map/ppermute | solution.py:17
  365.3 5.6 %collective-permute-start.4 = (f32[6400]{0:T(1024)}, f32[6400]{0:T(1024)}, u32[]{:S(2)}, u32[]{:S(2)}) collective-permute-start(f32[6400]{0:T(1024)} %reshape.224), channel_id=1, source_target_pairs={{0,16},{1,17},{2,18},{3,19},{4,20},{5,21},{6,22},{7,23},{8,24},{9,... | collective-permute-start | bytes 76808 | tf_op jit(solution)/shard_map/ppermute | solution.py:17
  374.5 1.9 broadcast_in_dim.526
  377.6 1.9 broadcast_in_dim.506
  380.2 1.9 broadcast_in_dim.518
  382.9 1.9 broadcast_in_dim.514
  385.5 1.9 broadcast_in_dim.546
  387.6 1.6 broadcast_in_dim.483
  389.2 3.8 broadcast_in_dim.484
  393.2 13.5 %fusion.61 = f32[10,10,10,1,384]{4,2,1,0,3:T(8,128)S(1)} fusion(f32[10,10,10,384]{3,2,1,0:T(8,128)S(1)} %copy-done.3, f32[]{:T(128)} %bitcast.61, f32[10,384]{1,0:T(8,128)S(1)} %copy-done.17, f32[]{:T(128)} %bitcast.58, f32[10,384]{1,0:T(8,128)S(1)} %copy-done.21, f32[10,10,384]{2,1,0:T(8,128)} %broadcast_in_dim.546, f32[10,384]{1,0:T(8,128)S(1)} %copy-done.22, ...), kind=kOutput, calls=%fused_computation.94 | convolution fusion | flops 1811859456 | bytes 5103412 | tf_op jit(solution)/shard_map/abcj,ij->abci/dot_general | solution.py:185
  406.7 2.7 copy.32
  (230 shorter events, 48.7 us)
Async XLA Ops:
  46.9 5.1 %copy-start.30 = (s32[1,384]{1,0:T(1,128)S(1)}, s32[1,384]{1,0:T(1,128)}, u32[]{:S(2)}) copy-start(s32[1,384]{1,0:T(1,128)} %param.6) | copy-start | bytes 4612
  46.9 31.2 %all-to-all-start.2 = ((f32[5,10,10,2,384]{4,2,1,0,3:T(8,128)}), f32[5,10,10,2,384]{4,2,1,0,3:T(8,128)S(1)}, u32[]{:S(2)}, u32[]{:S(2)}) async-start(f32[5,10,10,2,384]{4,2,1,0,3:T(8,128)} %get-tuple-element.46), calls=%async_computation.2 | async-start | bytes 4915200 | tf_op jit(solution)/shard_map/all_to_all | solution.py:154
  52.0 65.6 %copy-start.28 = (s32[384]{0:T(512)}, s32[384]{0:T(512)S(1)}, u32[]{:S(2)}) copy-start(s32[384]{0:T(512)S(1)} %reduce) | copy-start | bytes 4612
  56.3 148.2 %copy-start.24 = (pred[10]{0:T(512)(128)(4,1)}, pred[10]{0:T(512)(128)(4,1)S(1)}, u32[]{:S(2)}) copy-start(pred[10]{0:T(512)(128)(4,1)S(1)} %iota_compare_fusion.6) | copy-start | bytes 34
  78.1 31.9 %all-to-all-start = ((f32[5,10,10,2,384]{4,2,1,0,3:T(8,128)}), f32[5,10,10,2,384]{4,2,1,0,3:T(8,128)}, u32[]{:S(2)}, u32[]{:S(2)}) async-start(f32[5,10,10,2,384]{4,2,1,0,3:T(8,128)} %get-tuple-element.44), calls=%async_computation | async-start | bytes 4915200 | tf_op jit(solution)/shard_map/all_to_all | solution.py:152
  84.7 119.8 %copy-start.26 = (pred[10]{0:T(512)(128)(4,1)}, pred[10]{0:T(512)(128)(4,1)S(1)}, u32[]{:S(2)}) copy-start(pred[10]{0:T(512)(128)(4,1)S(1)} %iota_compare_fusion.5) | copy-start | bytes 34
  120.6 15.4 %copy-start.2 = (f32[10,10,10,384]{3,2,1,0:T(8,128)}, f32[10,10,10,384]{3,2,1,0:T(8,128)S(1)}, u32[]{:S(2)}) copy-start(f32[10,10,10,384]{3,2,1,0:T(8,128)S(1)} %fusion.38) | copy-start | bytes 4608004
  147.2 33.7 %slice-start = ((s8[24576000]{0:T(1024)(128)(4,1)}), s8[4194304]{0:T(1024)(128)(4,1)S(1)}, s32[]{:S(2)}) async-start(s8[24576000]{0:T(1024)(128)(4,1)} %bitcast.222), calls=%async_computation.3 | async-start | bytes 8388608
  147.2 33.8 %slice-start.1 = ((s8[24576000]{0:T(1024)(128)(4,1)}), s8[4194304]{0:T(1024)(128)(4,1)S(1)}, s32[]{:S(2)}) async-start(s8[24576000]{0:T(1024)(128)(4,1)} %bitcast.222), calls=%async_computation.4 | async-start | bytes 8388608
  147.2 33.8 %slice-start.2 = ((s8[24576000]{0:T(1024)(128)(4,1)}), s8[4194304]{0:T(1024)(128)(4,1)S(1)}, s32[]{:S(2)}) async-start(s8[24576000]{0:T(1024)(128)(4,1)} %bitcast.222), calls=%async_computation.5 | async-start | bytes 8388608
  147.2 33.8 %slice-start.3 = ((s8[24576000]{0:T(1024)(128)(4,1)}), s8[4194304]{0:T(1024)(128)(4,1)S(1)}, s32[]{:S(2)}) async-start(s8[24576000]{0:T(1024)(128)(4,1)} %bitcast.222), calls=%async_computation.6 | async-start | bytes 8388608
  147.2 33.8 %slice-start.4 = ((s8[24576000]{0:T(1024)(128)(4,1)}), s8[4194304]{0:T(1024)(128)(4,1)S(1)}, s32[]{:S(2)}) async-start(s8[24576000]{0:T(1024)(128)(4,1)} %bitcast.222), calls=%async_computation.7 | async-start | bytes 8388608
  174.1 6.9 %slice-start.5 = ((s8[24576000]{0:T(1024)(128)(4,1)}), s8[3604480]{0:T(1024)(128)(4,1)S(1)}, s32[]{:S(2)}) async-start(s8[24576000]{0:T(1024)(128)(4,1)} %bitcast.222), calls=%async_computation.8 | async-start | bytes 7208960
  232.8 7.3 %copy-start.6 = (f32[1,10,10,6,8,8]{5,4,3,0,2,1:T(8,128)S(1)}, f32[1,10,10,6,8,8]{5,4,3,0,2,1:T(8,128)}, u32[]{:S(2)}) copy-start(f32[1,10,10,6,8,8]{5,4,3,0,2,1:T(8,128)} %get-tuple-element.62) | copy-start | bytes 460804
  241.3 7.0 %copy-start.4 = (f32[10,1,10,6,8,8]{5,4,3,2,1,0:T(8,128)S(1)}, f32[10,1,10,6,8,8]{5,4,3,2,1,0:T(8,128)}, u32[]{:S(2)}) copy-start(f32[10,1,10,6,8,8]{5,4,3,2,1,0:T(8,128)} %get-tuple-element.65) | copy-start | bytes 460804
  256.1 31.6 %copy-start.8 = (f32[1,10,10,1,8,8]{5,4,3,2,1,0:T(8,128)S(1)}, f32[1,10,10,1,8,8]{5,4,3,2,1,0:T(8,128)}, u32[]{:S(2)}) copy-start(f32[1,10,10,1,8,8]{5,4,3,2,1,0:T(8,128)} %get-tuple-element.30) | copy-start | bytes 76804
  256.1 32.5 %collective-permute-start = (f32[1]{0:T(128)}, f32[1]{0:T(128)}, u32[]{:S(2)}, u32[]{:S(2)}) collective-permute-start(f32[1]{0:T(128)} %bitcast.39), channel_id=1, source_target_pairs={{0,21},{1,22},{2,23},{3,24},{4,25},{5,26},{6,27},{7,28},{8,29},{9,... | collective-permute-start | bytes 20 | tf_op jit(solution)/shard_map/ppermute | solution.py:17
  265.9 24.5 %collective-permute-start.25 = (f32[1]{0:T(128)}, f32[1]{0:T(128)}, u32[]{:S(2)}, u32[]{:S(2)}) collective-permute-start(f32[1]{0:T(128)} %bitcast.60), channel_id=1, source_target_pairs={{21,0},{22,1},{23,2},{24,3},{25,4},{26,5},{27,6},{28,7},{29,8},{30... | collective-permute-start | bytes 20 | tf_op jit(solution)/shard_map/ppermute | solution.py:17
  267.2 30.4 %collective-permute-start.19 = (f32[1]{0:T(128)}, f32[1]{0:T(128)}, u32[]{:S(2)}, u32[]{:S(2)}) collective-permute-start(f32[1]{0:T(128)} %bitcast.54), channel_id=1, source_target_pairs={{13,0},{14,1},{15,2},{16,3},{17,4},{18,5},{19,6},{20,7},{21,8},{22... | collective-permute-start | bytes 20 | tf_op jit(solution)/shard_map/ppermute | solution.py:17
  268.5 32.6 %collective-permute-start.17 = (f32[1]{0:T(128)}, f32[1]{0:T(128)}, u32[]{:S(2)}, u32[]{:S(2)}) collective-permute-start(f32[1]{0:T(128)} %bitcast.51), channel_id=1, source_target_pairs={{11,0},{12,1},{13,2},{14,3},{15,4},{16,5},{17,6},{18,7},{19,8},{20... | collective-permute-start | bytes 20 | tf_op jit(solution)/shard_map/ppermute | solution.py:17
  269.8 33.9 %collective-permute-start.8 = (f32[1]{0:T(128)}, f32[1]{0:T(128)}, u32[]{:S(2)}, u32[]{:S(2)}) collective-permute-start(f32[1]{0:T(128)} %bitcast.48), channel_id=1, source_target_pairs={{0,11},{1,12},{2,13},{3,14},{4,15},{5,16},{6,17},{7,18},{8,19},{9,... | collective-permute-start | bytes 20 | tf_op jit(solution)/shard_map/ppermute | solution.py:17
  288.6 19.4 %collective-permute-start.23 = (f32[1]{0:T(128)}, f32[1]{0:T(128)}, u32[]{:S(2)}, u32[]{:S(2)}) collective-permute-start(f32[1]{0:T(128)} %bitcast.57), channel_id=1, source_target_pairs={{19,0},{20,1},{21,2},{22,3},{23,4},{24,5},{25,6},{26,7},{27,8},{28... | collective-permute-start | bytes 20 | tf_op jit(solution)/shard_map/ppermute | solution.py:17
  290.4 20.1 %collective-permute-start.6 = (f32[1]{0:T(128)}, f32[1]{0:T(128)}, u32[]{:S(2)}, u32[]{:S(2)}) collective-permute-start(f32[1]{0:T(128)} %bitcast.45), channel_id=1, source_target_pairs={{0,13},{1,14},{2,15},{3,16},{4,17},{5,18},{6,19},{7,20},{8,21},{9,... | collective-permute-start | bytes 20 | tf_op jit(solution)/shard_map/ppermute | solution.py:17
  297.6 18.1 %collective-permute-start.2 = (f32[1]{0:T(128)}, f32[1]{0:T(128)}, u32[]{:S(2)}, u32[]{:S(2)}) collective-permute-start(f32[1]{0:T(128)} %bitcast.42), channel_id=1, source_target_pairs={{0,19},{1,20},{2,21},{3,22},{4,23},{5,24},{6,25},{7,26},{8,27},{9,... | collective-permute-start | bytes 20 | tf_op jit(solution)/shard_map/ppermute | solution.py:17
  301.1 17.0 %collective-permute-start.11 = (f32[60]{0:T(128)S(1)}, f32[60]{0:T(128)S(1)}, u32[]{:S(2)}, u32[]{:S(2)}) collective-permute-start(f32[60]{0:T(128)S(1)} %reshape.231), channel_id=1, source_target_pairs={{0,3},{1,4},{2,5},{3,6},{4,7},{5,8},{6,9},{7,10},{8,11},{9,12},{10... | collective-permute-start | bytes 728 | tf_op jit(solution)/shard_map/ppermute | solution.py:17
  303.7 15.7 %collective-permute-start.14 = (f32[60]{0:T(128)S(1)}, f32[60]{0:T(128)S(1)}, u32[]{:S(2)}, u32[]{:S(2)}) collective-permute-start(f32[60]{0:T(128)S(1)} %reshape.234), channel_id=1, source_target_pairs={{3,0},{4,1},{5,2},{6,3},{7,4},{8,5},{9,6},{10,7},{11,8},{12,9},{13... | collective-permute-start | bytes 728 | tf_op jit(solution)/shard_map/ppermute | solution.py:17
  308.0 12.8 %collective-permute-start.16 = (f32[60]{0:T(128)S(1)}, f32[60]{0:T(128)S(1)}, u32[]{:S(2)}, u32[]{:S(2)}) collective-permute-start(f32[60]{0:T(128)S(1)} %reshape.236), channel_id=1, source_target_pairs={{5,0},{6,1},{7,2},{8,3},{9,4},{10,5},{11,6},{12,7},{13,8},{14,9},{... | collective-permute-start | bytes 728 | tf_op jit(solution)/shard_map/ppermute | solution.py:17
  310.5 18.4 %collective-permute-start.9 = (f32[60]{0:T(128)S(1)}, f32[60]{0:T(128)S(1)}, u32[]{:S(2)}, u32[]{:S(2)}) collective-permute-start(f32[60]{0:T(128)S(1)} %reshape.229), channel_id=1, source_target_pairs={{0,5},{1,6},{2,7},{3,8},{4,9},{5,10},{6,11},{7,12},{8,13},{9,14},{... | collective-permute-start | bytes 728 | tf_op jit(solution)/shard_map/ppermute | solution.py:17
  315.7 18.1 %collective-permute-start.5 = (f32[80]{0:T(128)S(1)}, f32[80]{0:T(128)S(1)}, u32[]{:S(2)}, u32[]{:S(2)}) collective-permute-start(f32[80]{0:T(128)S(1)} %reshape.225), channel_id=1, source_target_pairs={{0,15},{1,16},{2,17},{3,18},{4,19},{5,20},{6,21},{7,22},{8,23},{9,... | collective-permute-start | bytes 968 | tf_op jit(solution)/shard_map/ppermute | solution.py:17
  318.2 17.0 %collective-permute-start.20 = (f32[80]{0:T(128)S(1)}, f32[80]{0:T(128)S(1)}, u32[]{:S(2)}, u32[]{:S(2)}) collective-permute-start(f32[80]{0:T(128)S(1)} %reshape.240), channel_id=1, source_target_pairs={{15,0},{16,1},{17,2},{18,3},{19,4},{20,5},{21,6},{22,7},{23,8},{24... | collective-permute-start | bytes 968 | tf_op jit(solution)/shard_map/ppermute | solution.py:17
  319.5 17.0 %collective-permute-start.22 = (f32[80]{0:T(128)S(1)}, f32[80]{0:T(128)S(1)}, u32[]{:S(2)}, u32[]{:S(2)}) collective-permute-start(f32[80]{0:T(128)S(1)} %reshape.242), channel_id=1, source_target_pairs={{17,0},{18,1},{19,2},{20,3},{21,4},{22,5},{23,6},{24,7},{25,8},{26... | collective-permute-start | bytes 968 | tf_op jit(solution)/shard_map/ppermute | solution.py:17
  320.8 22.4 %collective-permute-start.3 = (f32[80]{0:T(128)S(1)}, f32[80]{0:T(128)S(1)}, u32[]{:S(2)}, u32[]{:S(2)}) collective-permute-start(f32[80]{0:T(128)S(1)} %reshape.223), channel_id=1, source_target_pairs={{0,17},{1,18},{2,19},{3,20},{4,21},{5,22},{6,23},{7,24},{8,25},{9,... | collective-permute-start | bytes 968 | tf_op jit(solution)/shard_map/ppermute | solution.py:17
  328.9 16.2 %collective-permute-start.7 = (f32[80]{0:T(128)S(1)}, f32[80]{0:T(128)S(1)}, u32[]{:S(2)}, u32[]{:S(2)}) collective-permute-start(f32[80]{0:T(128)S(1)} %reshape.227), channel_id=1, source_target_pairs={{0,12},{1,13},{2,14},{3,15},{4,16},{5,17},{6,18},{7,19},{8,20},{9,... | collective-permute-start | bytes 968 | tf_op jit(solution)/shard_map/ppermute | solution.py:17
  333.8 16.8 %collective-permute-start.18 = (f32[80]{0:T(128)S(1)}, f32[80]{0:T(128)S(1)}, u32[]{:S(2)}, u32[]{:S(2)}) collective-permute-start(f32[80]{0:T(128)S(1)} %reshape.238), channel_id=1, source_target_pairs={{12,0},{13,1},{14,2},{15,3},{16,4},{17,5},{18,6},{19,7},{20,8},{21... | collective-permute-start | bytes 968 | tf_op jit(solution)/shard_map/ppermute | solution.py:17
  335.2 17.4 %collective-permute-start.24 = (f32[80]{0:T(128)S(1)}, f32[80]{0:T(128)S(1)}, u32[]{:S(2)}, u32[]{:S(2)}) collective-permute-start(f32[80]{0:T(128)S(1)} %reshape.244), channel_id=1, source_target_pairs={{20,0},{21,1},{22,2},{23,3},{24,4},{25,5},{26,6},{27,7},{28,8},{29... | collective-permute-start | bytes 968 | tf_op jit(solution)/shard_map/ppermute | solution.py:17
  336.5 20.4 %collective-permute-start.1 = (f32[80]{0:T(128)S(1)}, f32[80]{0:T(128)S(1)}, u32[]{:S(2)}, u32[]{:S(2)}) collective-permute-start(f32[80]{0:T(128)S(1)} %reshape.221), channel_id=1, source_target_pairs={{0,20},{1,21},{2,22},{3,23},{4,24},{5,25},{6,26},{7,27},{8,28},{9,... | collective-permute-start | bytes 968 | tf_op jit(solution)/shard_map/ppermute | solution.py:17
  343.2 22.1 %collective-permute-start.13 = (f32[4800]{0:T(1024)S(1)}, f32[4800]{0:T(1024)S(1)}, u32[]{:S(2)}, u32[]{:S(2)}) collective-permute-start(f32[4800]{0:T(1024)S(1)} %reshape.233), channel_id=1, source_target_pairs={{1,0},{2,1},{3,2},{4,3},{5,4},{6,5},{7,6},{8,7},{9,8},{10,9},{11,1... | collective-permute-start | bytes 57608 | tf_op jit(solution)/shard_map/ppermute | solution.py:17
  345.2 25.8 %collective-permute-start.12 = (f32[4800]{0:T(1024)S(1)}, f32[4800]{0:T(1024)S(1)}, u32[]{:S(2)}, u32[]{:S(2)}) collective-permute-start(f32[4800]{0:T(1024)S(1)} %reshape.232), channel_id=1, source_target_pairs={{0,1},{1,2},{2,3},{3,4},{4,5},{5,6},{6,7},{7,8},{8,9},{9,10},{10,1... | collective-permute-start | bytes 57608 | tf_op jit(solution)/shard_map/ppermute | solution.py:17
  350.6 20.4 %collective-permute-start.15 = (f32[4800]{0:T(1024)S(1)}, f32[4800]{0:T(1024)S(1)}, u32[]{:S(2)}, u32[]{:S(2)}) collective-permute-start(f32[4800]{0:T(1024)S(1)} %reshape.235), channel_id=1, source_target_pairs={{4,0},{5,1},{6,2},{7,3},{8,4},{9,5},{10,6},{11,7},{12,8},{13,9},{1... | collective-permute-start | bytes 57608 | tf_op jit(solution)/shard_map/ppermute | solution.py:17
  352.6 18.4 %collective-permute-start.10 = (f32[4800]{0:T(1024)S(1)}, f32[4800]{0:T(1024)S(1)}, u32[]{:S(2)}, u32[]{:S(2)}) collective-permute-start(f32[4800]{0:T(1024)S(1)} %reshape.230), channel_id=1, source_target_pairs={{0,4},{1,5},{2,6},{3,7},{4,8},{5,9},{6,10},{7,11},{8,12},{9,13},{1... | collective-permute-start | bytes 57608 | tf_op jit(solution)/shard_map/ppermute | solution.py:17
  356.9 28.2 %collective-permute-start.21 = (f32[6400]{0:T(1024)}, f32[6400]{0:T(1024)S(1)}, u32[]{:S(2)}, u32[]{:S(2)}) collective-permute-start(f32[6400]{0:T(1024)} %reshape.241), channel_id=1, source_target_pairs={{16,0},{17,1},{18,2},{19,3},{20,4},{21,5},{22,6},{23,7},{24,8},{25... | collective-permute-start | bytes 76808 | tf_op jit(solution)/shard_map/ppermute | solution.py:17
  365.3 19.5 %collective-permute-start.4 = (f32[6400]{0:T(1024)}, f32[6400]{0:T(1024)}, u32[]{:S(2)}, u32[]{:S(2)}) collective-permute-start(f32[6400]{0:T(1024)} %reshape.224), channel_id=1, source_target_pairs={{0,16},{1,17},{2,18},{3,19},{4,20},{5,21},{6,22},{7,23},{8,24},{9,... | collective-permute-start | bytes 76808 | tf_op jit(solution)/shard_map/ppermute | solution.py:17
  387.4 5.5 %copy-start.3 = (f32[10,10,10,384]{3,2,1,0:T(8,128)S(1)}, f32[10,10,10,384]{3,2,1,0:T(8,128)}, u32[]{:S(2)}) copy-start(f32[10,10,10,384]{3,2,1,0:T(8,128)} %copy-done.2) | copy-start | bytes 4608004
  387.4 5.5 %copy-start.9 = (f32[10,10,384]{2,1,0:T(8,128)S(1)}, f32[10,10,384]{2,1,0:T(8,128)}, u32[]{:S(2)}) copy-start(f32[10,10,384]{2,1,0:T(8,128)} %broadcast_in_dim.442) | copy-start | bytes 460804
  387.4 5.6 %copy-start.12 = (f32[10,384]{1,0:T(8,128)S(1)}, f32[10,384]{1,0:T(8,128)}, u32[]{:S(2)}) copy-start(f32[10,384]{1,0:T(8,128)} %broadcast_in_dim.501) | copy-start | bytes 46084
  387.4 5.6 %copy-start.13 = (f32[10,384]{1,0:T(8,128)S(1)}, f32[10,384]{1,0:T(8,128)}, u32[]{:S(2)}) copy-start(f32[10,384]{1,0:T(8,128)} %broadcast_in_dim.530) | copy-start | bytes 46084
  387.4 5.6 %copy-start.14 = (f32[10,384]{1,0:T(8,128)S(1)}, f32[10,384]{1,0:T(8,128)}, u32[]{:S(2)}) copy-start(f32[10,384]{1,0:T(8,128)} %broadcast_in_dim.522) | copy-start | bytes 46084
  387.5 5.6 %copy-start.15 = (f32[10,384]{1,0:T(8,128)S(1)}, f32[10,384]{1,0:T(8,128)}, u32[]{:S(2)}) copy-start(f32[10,384]{1,0:T(8,128)} %broadcast_in_dim.510) | copy-start | bytes 46084
  387.5 5.6 %copy-start.16 = (f32[10,384]{1,0:T(8,128)S(1)}, f32[10,384]{1,0:T(8,128)}, u32[]{:S(2)}) copy-start(f32[10,384]{1,0:T(8,128)} %broadcast_in_dim.473) | copy-start | bytes 46084
  387.5 5.6 %copy-start.17 = (f32[10,384]{1,0:T(8,128)S(1)}, f32[10,384]{1,0:T(8,128)}, u32[]{:S(2)}) copy-start(f32[10,384]{1,0:T(8,128)} %broadcast_in_dim.556) | copy-start | bytes 46084
  387.5 5.6 %copy-start.18 = (f32[10,384]{1,0:T(8,128)S(1)}, f32[10,384]{1,0:T(8,128)}, u32[]{:S(2)}) copy-start(f32[10,384]{1,0:T(8,128)} %broadcast_in_dim.536) | copy-start | bytes 46084
  387.5 5.6 %copy-start.25 = (pred[10]{0:T(512)(128)(4,1)S(1)}, pred[10]{0:T(512)(128)(4,1)}, u32[]{:S(2)}) copy-start(pred[10]{0:T(512)(128)(4,1)} %copy-done.24) | copy-start | bytes 34
  387.5 5.6 %copy-start.27 = (pred[10]{0:T(512)(128)(4,1)S(1)}, pred[10]{0:T(512)(128)(4,1)}, u32[]{:S(2)}) copy-start(pred[10]{0:T(512)(128)(4,1)} %copy-done.26) | copy-start | bytes 34
  387.5 5.6 %copy-start.29 = (s32[384]{0:T(512)S(1)}, s32[384]{0:T(512)}, u32[]{:S(2)}) copy-start(s32[384]{0:T(512)} %copy-done.28) | copy-start | bytes 4612
  387.5 5.6 %copy-start.31 = (pred[384]{0:T(512)(128)(4,1)S(1)}, pred[384]{0:T(512)(128)(4,1)}, u32[]{:S(2)}) copy-start(pred[384]{0:T(512)(128)(4,1)} %iota.888) | copy-start | bytes 1156
  387.5 5.6 %copy-start.32 = (pred[384]{0:T(512)(128)(4,1)S(1)}, pred[384]{0:T(512)(128)(4,1)}, u32[]{:S(2)}) copy-start(pred[384]{0:T(512)(128)(4,1)} %iota.868) | copy-start | bytes 1156
  387.5 5.6 %copy-start.33 = (pred[384]{0:T(512)(128)(4,1)S(1)}, pred[384]{0:T(512)(128)(4,1)}, u32[]{:S(2)}) copy-start(pred[384]{0:T(512)(128)(4,1)} %iota.884) | copy-start | bytes 1156
  389.2 4.0 copy-start.20
  389.2 4.0 copy-start.21
  389.2 4.0 copy-start.22
  389.2 4.0 copy-start.23
  389.2 4.0 copy-start.34
  389.2 4.0 copy-start.35
  389.2 4.0 copy-start.36
  (9 other events, 24.9 us)
where the time goes:
time: 417 us; the launch traced here: 410 us
  local copies, waits for them, and re-layouts  148 us (35%)
  starting transfers between devices  98.2 us (24%)
  other arithmetic  57.4 us (14%)
  waiting for transfers between devices  37.5 us (9%)
  matrix products  31.4 us (8%)
  blocking collectives  30.7 us (7%)
  between operations  6.53 us (2%)
    ppermute x26, starting transfers between devices, passed_along(): return lax.ppermute(x, axis, pairs)  86.5 us
    add x3, other arithmetic, local_pass(): return field + jnp.where(node_iota == last_node, add_upper, 0.0)  52.7 us
    broadcast_in_dim x54, local copies, waits for them, and re-layouts, add_region(): jnp.where(region_mask(field.shape, offset, block_grid), values, 0.0)  32.5 us
    all_to_all x1, blocking collectives, body(): lax.all_to_all(fluxes[1], 'comp', split_axis=3, concat_axis=0, tiled=True)  30.7 us
    all_to_all x1, waiting for transfers between devices, body(): lax.all_to_all(fluxes[2], 'comp', split_axis=3, concat_axis=0, tiled=True)  21.8 us
    slice x7, local copies, waits for them, and re-layouts, take_region(): return field[nodes_key + elems_key]  18.2 us
    all_to_all x1, waiting for transfers between devices, body(): lax.all_to_all(fluxes[0], 'comp', split_axis=3, concat_axis=0, tiled=True)  15.7 us
    reshape x1, local copies, waits for them, and re-layouts, body(): canonical.reshape((node_count, node_count, node_count) + block_grid)  15.3 us
  transfers between devices with their start and end apart: 28, of which 2 were waited for; matrix products, arithmetic and copies ran while one was open for 12% of the time, Pallas kernels for 0%

commit v1 on v0

--- a/solution.py
+++ b/solution.py
@@ -9,6 +9,13 @@
 BLOCK_Z = 8
 GRID_Y = 4
 exact_mode = lax.Precision.HIGHEST
+
+
+def trade_parts(x, mesh_axis, split, join):
+    n_dev = lax.axis_size(mesh_axis)
+    blocks = jnp.stack(jnp.split(x, n_dev, axis=split), axis=0)
+    blocks = lax.all_to_all(blocks, mesh_axis, split_axis=0, concat_axis=0)
+    return jnp.concatenate(blocks, axis=join)
 
 
 def passed_along(x, axis, by):
@@ -149,7 +156,7 @@
             + geometry[2, direction] * velocity[2]
         )
     flux_r, flux_s, flux_t = (
-        lax.all_to_all(fluxes[0], "comp", split_axis=3, concat_axis=0, tiled=True),
+        trade_parts(fluxes[0], "comp", 3, 0),
         lax.all_to_all(fluxes[1], "comp", split_axis=3, concat_axis=0, tiled=True),
         lax.all_to_all(fluxes[2], "comp", split_axis=3, concat_axis=0, tiled=True),
     )

time: 417 us -> 403 us (0.966)
  blocking collectives: 30.7 us -> 0 us
  waiting for transfers between devices: 37.5 us -> 45.9 us
  other arithmetic: 57.4 us -> 65.5 us
  starting transfers between devices: 98.2 us -> 103 us
    all_to_all x1 -> x0, blocking collectives: 30.7 us -> none  [body(): lax.all_to_all(fluxes[1], 'comp', split_axis=3, concat_axis=0, tiled=True)]
    slice x2 -> x0, local copies, waits for them, and re-layouts: 11.7 us -> none  [the longest x1 7.84 us: body(): geometry[0, direction] * velocity[0] + geometry[1, direction] * velocity[1]]
    all_to_all x1 -> x2, waiting for transfers between devices: 15.7 us -> 22.1 us  [the longest x1 16.2 us: body(): lax.all_to_all(fluxes[1], 'comp', split_axis=3, concat_axis=0, tiled=True)]
    all_to_all x1 -> x2, starting transfers between devices: 6.57 us -> 12.4 us  [the longest x1 6.2 us: trade_parts(): blocks = lax.all_to_all(blocks, mesh_axis, split_axis=0, concat_axis=0)]
    add x1, other arithmetic: 4.47 us -> 9.91 us  [body(): geometry[0, direction] * velocity[0] + geometry[1, direction] * velocity[1]]
    add x0 -> x2, local copies, waits for them, and re-layouts: none -> 4.86 us  [body(): geometry[0, direction] * velocity[0] + geometry[1, direction] * velocity[1]]
  transfers between devices with their start and end apart: 28 -> 29, of which waited for: 2 -> 3; matrix products, arithmetic and copies ran while one was open for 12% -> 15% of each run, Pallas kernels for 0% -> 0%
where the time goes in v1:
time: 403 us; the launch traced here: 396 us
  local copies, waits for them, and re-layouts  146 us (36%)
  starting transfers between devices  103 us (26%)
  other arithmetic  65.5 us (16%)
  waiting for transfers between devices  45.9 us (11%)
  matrix products  29.9 us (7%)
  between operations  6.44 us (2%)
    ppermute x26, starting transfers between devices, passed_along(): return lax.ppermute(x, axis, pairs)  86.4 us
    add x3, other arithmetic, local_pass(): return field + jnp.where(node_iota == last_node, add_upper, 0.0)  52.8 us
    broadcast_in_dim x54, local copies, waits for them, and re-layouts, add_region(): jnp.where(region_mask(field.shape, offset, block_grid), values, 0.0)  32.5 us
    all_to_all x1, waiting for transfers between devices, body(): lax.all_to_all(fluxes[2], 'comp', split_axis=3, concat_axis=0, tiled=True)  23.8 us
    slice x7, local copies, waits for them, and re-layouts, take_region(): return field[nodes_key + elems_key]  18.2 us
    all_to_all x1, waiting for transfers between devices, body(): lax.all_to_all(fluxes[1], 'comp', split_axis=3, concat_axis=0, tiled=True)  16.2 us
    reshape x1, local copies, waits for them, and re-layouts, body(): canonical.reshape((node_count, node_count, node_count) + block_grid)  15.4 us
    dot_general x1, matrix products, body(): jnp.einsum('abcj,ij->abci', assembled, place_matrix, precision=exact_mode)  13.5 us
  transfers between devices with their start and end apart: 29, of which 3 were waited for; matrix products, arithmetic and copies ran while one was open for 15% of the time, Pallas kernels for 0%

profile of v1, /device:TPU:7, one launch (start us, length us, event | category | flops | bytes accessed | tf_op | source)
XLA Modules:
  0.0 396.4 jit_solution(5952678448692855398)
XLA Ops:
  0.0 9.9 %fusion.55 = (f32[5,10,10,2,384]{4,3,2,1,0:T(2,128)}, f32[5,10,10,2,384]{4,3,2,1,0:T(2,128)S(1)}, f32[5,10,10,2,384]{4,3,2,1,0:T(2,128)}) fusion(f32[3,3,5,10,10,2,384]{6,5,4,3,2,1,0:T(2,128)} %param.5, f32[3,5,10,10,2,384]{5,4,3,2,1,0:T(2,128)} %param.4), kind=kLoop, calls=%fused_computation.80 | loop fusion | flops 5760000 | bytes 23040000 | tf_op jit(solution)/shard_map/add | solution.py:154
  9.9 1.7 copy.45
  11.6 4.1 %all-to-all-start.2 = ((f32[5,10,10,2,384]{4,2,1,0,3:T(8,128)}), f32[5,10,10,2,384]{4,2,1,0,3:T(8,128)S(1)}, u32[]{:S(2)}, u32[]{:S(2)}) async-start(f32[5,10,10,2,384]{4,2,1,0,3:T(8,128)} %copy.45), calls=%async_computation.2 | async-start | bytes 4915200 | tf_op jit(solution)/shard_map/all_to_all | solution.py:161
  15.7 3.2 copy.42
  18.9 23.8 %all-to-all-done.2 = f32[5,10,10,2,384]{4,2,1,0,3:T(8,128)S(1)} async-done(((f32[5,10,10,2,384]{4,2,1,0,3:T(8,128)}), f32[5,10,10,2,384]{4,2,1,0,3:T(8,128)S(1)}, u32[]{:S(2)}, u32[]{:S(2)}) %all-to-all-start.2) | async-done | bytes 1536032 | tf_op jit(solution)/shard_map/all_to_all | solution.py:161
  42.6 6.2 %all-to-all-start.1 = ((f32[5,10,10,2,384]{4,2,1,0,3:T(8,128)}), f32[5,10,10,2,384]{4,2,1,0,3:T(8,128)}, u32[]{:S(2)}, u32[]{:S(2)}) async-start(f32[5,10,10,2,384]{4,2,1,0,3:T(8,128)} %copy.42), calls=%async_computation.1 | async-start | bytes 4915200 | tf_op jit(solution)/shard_map/all_to_all | solution.py:160
  53.0 3.2 slice_bitcast_fusion.1
  56.2 2.6 pad_maximum_fusion
  58.8 16.2 %all-to-all-done.1 = f32[5,10,10,2,384]{4,2,1,0,3:T(8,128)} async-done(((f32[5,10,10,2,384]{4,2,1,0,3:T(8,128)}), f32[5,10,10,2,384]{4,2,1,0,3:T(8,128)}, u32[]{:S(2)}, u32[]{:S(2)}) %all-to-all-start.1) | async-done | bytes 1536032 | tf_op jit(solution)/shard_map/all_to_all | solution.py:160
  75.0 6.2 %all-to-all-start = ((f32[2,5,10,10,1,384]{5,4,3,2,1,0:T(1,128)}), f32[2,5,10,10,1,384]{5,4,3,2,1,0:T(1,128)}, u32[]{:S(2)}, u32[]{:S(2)}) async-start(f32[2,5,10,10,1,384]{5,4,3,2,1,0:T(1,128)} %pad_maximum_fusion), calls=%async_computation | async-start | bytes 3072000 | tf_op jit(solution)/shard_map/all_to_all | solution.py:17
  81.2 2.2 copy.43
  83.5 3.6 fusion.120
  87.1 3.7 fusion.119
  90.8 5.9 %all-to-all-done = f32[2,5,10,10,1,384]{5,4,3,2,1,0:T(1,128)} async-done(((f32[2,5,10,10,1,384]{5,4,3,2,1,0:T(1,128)}), f32[2,5,10,10,1,384]{5,4,3,2,1,0:T(1,128)}, u32[]{:S(2)}, u32[]{:S(2)}) %all-to-all-start) | async-done | bytes 1536032 | tf_op jit(solution)/shard_map/all_to_all | solution.py:17
  96.7 1.7 copy.51
  98.3 6.2 %fusion.22 = f32[10,10,10,384]{3,0,2,1:T(8,128)S(1)} fusion(f32[10,10,384,10]{2,3,1,0:T(8,128)S(1)} %copy-done.7, f32[10,10,384,10]{2,3,1,0:T(8,128)} %fusion.119, f32[10,10,1,1]{0,1,3,2:T(8,128)S(1)} %copy-done.12, f32[10,10,10,384]{3,2,1,0:T(8,128)S(1)} %bitcast.195), kind=kOutput, calls=%fused_computation.44 | convolution fusion | flops 46848000 | bytes 6144400 | tf_op jit(solution)/shard_map/ia,i...->a.../dot_general | solution.py:57
  104.5 2.9 fusion.23
  107.5 15.4 %reshape.220 = f32[10,10,10,6,8,8]{5,4,3,2,1,0:T(8,128)} reshape(f32[10,10,10,384]{3,2,1,0:T(8,128)S(1)} %fusion.23) | data formatting | bytes 3072000 | tf_op jit(solution)/shard_map/reshape | solution.py:172
  124.2 2.9 slice.174
  128.6 2.0 fusion.118
  130.7 2.0 fusion.117
  134.1 20.9 %select_add_fusion.2 = f32[10,10,10,6,8,8]{5,4,3,2,1,0:T(8,128)} fusion(f32[10,10,10,6,8,8]{5,4,3,2,1,0:T(8,128)} %reshape.220, f32[10,10,6,8,8]{4,3,2,1,0:T(8,128)S(1)} %get-tuple-element.51, f32[10,10,6,8,8]{4,3,2,1,0:T(8,128)S(1)} %get-tuple-element.49, pred[10]{0:T(512)(128)(4,1)S(1)} %iota_compare_fusion.5, pred[10]{0:T(512)(128)(4,1)S(1)} %iota_compare_fusion.6), kind=kLoop, calls=%fused_computation.2 | loop fusion | flops 1536000 | bytes 3379220 | tf_op jit(solution)/shard_map/add | solution.py:78
  155.0 5.9 %fusion.111 = (f32[10,1,10,6,7,8]{5,4,3,2,1,0:T(8,128)}, f32[10,1,10,6,7,8]{5,4,3,2,1,0:T(8,128)}) fusion(f32[10,10,10,6,8,8]{5,4,3,2,1,0:T(8,128)} %select_add_fusion.2), kind=kLoop, calls=%fused_computation.183 | loop fusion | bytes 537600 | tf_op jit(solution)/shard_map/slice | solution.py:74
  161.0 6.9 %fusion.112 = (f32[10,1,10,6,8,8]{5,4,3,2,1,0:T(8,128)}, f32[10,10,6,8,8]{4,3,2,1,0:T(8,128)}, f32[10,10,6,8,8]{4,3,2,1,0:T(8,128)}, f32[10,1,10,6,8,8]{5,4,3,2,1,0:T(8,128)}) fusion(f32[10,1,10,6,7,8]{5,4,3,2,1,0:T(8,128)} %get-tuple-element.33, f32[10,1,10,6,7,8]{5,4,3,2,1,0:T(8,128)} %get-tuple-element.34), kind=kLoop, calls=%fused_computation.184 | loop fusion | bytes 883200 | tf_op jit(solution)/shard_map/concatenate | solution.py:73
  167.9 14.5 %select_add_fusion.1 = f32[10,10,10,6,8,8]{5,4,3,2,1,0:T(8,128)} fusion(f32[10,10,6,8,8]{4,3,2,1,0:T(8,128)} %get-tuple-element.54, f32[10,10,6,8,8]{4,3,2,1,0:T(8,128)} %get-tuple-element.39, pred[10]{0:T(512)(128)(4,1)S(1)} %iota_compare_fusion.5, pred[10]{0:T(512)(128)(4,1)S(1)} %iota_compare_fusion.6, f32[10,10,6,8,8]{4,3,2,1,0:T(8,128)S(1)} %get-tuple-element.51, ...), kind=kLoop, calls=%fused_computation.1 | loop fusion | flops 3072000 | bytes 3686420 | tf_op jit(solution)/shard_map/add | solution.py:78
  182.4 3.3 fusion.110
  185.7 3.0 fusion.114
  188.7 2.7 fusion.115
  191.5 17.4 %select_add_fusion = f32[10,10,10,6,8,8]{5,4,3,2,1,0:T(8,128)} fusion(f32[10,10,6,8,8]{4,3,2,1,0:T(8,128)} %get-tuple-element.45, f32[10,10,6,8,8]{4,3,2,1,0:T(8,128)} %get-tuple-element.43, pred[10]{0:T(512)(128)(4,1)S(1)} %iota_compare_fusion.5, pred[10]{0:T(512)(128)(4,1)S(1)} %iota_compare_fusion.6, f32[10,10,6,8,8]{4,3,2,1,0:T(8,128)} %get-tuple-element.54, ...), kind=kLoop, calls=%fused_computation | loop fusion | flops 4608000 | bytes 3993620 | tf_op jit(solution)/shard_map/add | solution.py:78
  210.2 2.5 slice_reduce_fusion.11
  215.3 4.5 %slice_reduce_fusion.1 = (f32[10,10,6,8]{3,2,1,0:T(8,128)S(1)}, f32[10,10,6,8]{3,2,1,0:T(8,128)S(1)}) fusion(f32[10,10,10,6,8,8]{5,4,3,2,1,0:T(8,128)} %select_add_fusion), kind=kLoop, calls=%fused_computation.42 | loop fusion | bytes 76800 | tf_op jit(solution)/shard_map/slice | solution.py:103
  219.8 2.2 fusion.109
  222.0 5.0 %slice_reduce_fusion.3 = (f32[10,10,6,8]{3,2,1,0:T(8,128)}, f32[10,10,6,8]{3,2,1,0:T(8,128)}) fusion(f32[10,10,10,6,8,8]{5,4,3,2,1,0:T(8,128)} %select_add_fusion), kind=kLoop, calls=%fused_computation.134 | loop fusion | bytes 76800 | tf_op jit(solution)/shard_map/slice | solution.py:103
  228.3 3.6 broadcast_in_dim.442
  231.9 3.4 broadcast_in_dim.452
  235.3 1.9 broadcast_in_dim.454
  237.2 3.9 broadcast_in_dim.460
  241.2 1.9 broadcast_in_dim.462
  243.1 9.9 %collective-permute-start = (f32[1]{0:T(128)}, f32[1]{0:T(128)}, u32[]{:S(2)}, u32[]{:S(2)}) collective-permute-start(f32[1]{0:T(128)} %bitcast.38), channel_id=1, source_target_pairs={{0,21},{1,22},{2,23},{3,24},{4,25},{5,26},{6,27},{7,28},{8,29},{9,... | collective-permute-start | bytes 20 | tf_op jit(solution)/shard_map/ppermute | solution.py:24
  256.9 6.9 %collective-permute-start.8 = (f32[1]{0:T(128)}, f32[1]{0:T(128)}, u32[]{:S(2)}, u32[]{:S(2)}) collective-permute-start(f32[1]{0:T(128)} %bitcast.47), channel_id=1, source_target_pairs={{0,11},{1,12},{2,13},{3,14},{4,15},{5,16},{6,17},{7,18},{8,19},{9,... | collective-permute-start | bytes 20 | tf_op jit(solution)/shard_map/ppermute | solution.py:24
  271.8 1.8 reshape.225
  277.5 6.4 %collective-permute-start.6 = (f32[1]{0:T(128)}, f32[1]{0:T(128)}, u32[]{:S(2)}, u32[]{:S(2)}) collective-permute-start(f32[1]{0:T(128)} %bitcast.44), channel_id=1, source_target_pairs={{0,13},{1,14},{2,15},{3,16},{4,17},{5,18},{6,19},{7,20},{8,21},{9,... | collective-permute-start | bytes 20 | tf_op jit(solution)/shard_map/ppermute | solution.py:24
  284.5 3.0 collective-permute-start.2
  288.1 1.9 collective-permute-start.11
  290.7 3.6 collective-permute-start.14
  295.0 1.9 collective-permute-start.16
  297.5 4.5 %collective-permute-start.9 = (f32[60]{0:T(128)S(1)}, f32[60]{0:T(128)S(1)}, u32[]{:S(2)}, u32[]{:S(2)}) collective-permute-start(f32[60]{0:T(128)S(1)} %reshape.230), channel_id=1, source_target_pairs={{0,5},{1,6},{2,7},{3,8},{4,9},{5,10},{6,11},{7,12},{8,13},{9,14},{... | collective-permute-start | bytes 728 | tf_op jit(solution)/shard_map/ppermute | solution.py:24
  302.6 1.6 collective-permute-start.5
  307.6 7.9 %collective-permute-start.3 = (f32[80]{0:T(128)S(1)}, f32[80]{0:T(128)S(1)}, u32[]{:S(2)}, u32[]{:S(2)}) collective-permute-start(f32[80]{0:T(128)S(1)} %reshape.224), channel_id=1, source_target_pairs={{0,17},{1,18},{2,19},{3,20},{4,21},{5,22},{6,23},{7,24},{8,25},{9,... | collective-permute-start | bytes 968 | tf_op jit(solution)/shard_map/ppermute | solution.py:24
  323.3 6.7 %collective-permute-start.1 = (f32[80]{0:T(128)S(1)}, f32[80]{0:T(128)S(1)}, u32[]{:S(2)}, u32[]{:S(2)}) collective-permute-start(f32[80]{0:T(128)S(1)} %reshape.222), channel_id=1, source_target_pairs={{0,20},{1,21},{2,22},{3,23},{4,24},{5,25},{6,26},{7,27},{8,28},{9,... | collective-permute-start | bytes 968 | tf_op jit(solution)/shard_map/ppermute | solution.py:24
  330.0 1.9 collective-permute-start.13
  331.9 5.4 %collective-permute-start.12 = (f32[4800]{0:T(1024)S(1)}, f32[4800]{0:T(1024)S(1)}, u32[]{:S(2)}, u32[]{:S(2)}) collective-permute-start(f32[4800]{0:T(1024)S(1)} %reshape.233), channel_id=1, source_target_pairs={{0,1},{1,2},{2,3},{3,4},{4,5},{5,6},{6,7},{7,8},{8,9},{9,10},{10,1... | collective-permute-start | bytes 57608 | tf_op jit(solution)/shard_map/ppermute | solution.py:24
  337.4 1.9 collective-permute-start.15
  339.4 4.3 %collective-permute-start.10 = (f32[4800]{0:T(1024)S(1)}, f32[4800]{0:T(1024)S(1)}, u32[]{:S(2)}, u32[]{:S(2)}) collective-permute-start(f32[4800]{0:T(1024)S(1)} %reshape.231), channel_id=1, source_target_pairs={{0,4},{1,5},{2,6},{3,7},{4,8},{5,9},{6,10},{7,11},{8,12},{9,13},{1... | collective-permute-start | bytes 57608 | tf_op jit(solution)/shard_map/ppermute | solution.py:24
  352.1 5.6 %collective-permute-start.4 = (f32[6400]{0:T(1024)}, f32[6400]{0:T(1024)}, u32[]{:S(2)}, u32[]{:S(2)}) collective-permute-start(f32[6400]{0:T(1024)} %reshape.225), channel_id=1, source_target_pairs={{0,16},{1,17},{2,18},{3,19},{4,20},{5,21},{6,22},{7,23},{8,24},{9,... | collective-permute-start | bytes 76808 | tf_op jit(solution)/shard_map/ppermute | solution.py:24
  361.3 1.9 broadcast_in_dim.526
  364.4 1.9 broadcast_in_dim.506
  367.0 1.9 broadcast_in_dim.518
  369.7 1.9 broadcast_in_dim.514
  372.3 1.9 broadcast_in_dim.546
  374.3 1.6 broadcast_in_dim.483
  376.0 3.8 broadcast_in_dim.484
  380.0 13.5 %fusion.46 = f32[10,10,10,1,384]{4,2,1,0,3:T(8,128)S(1)} fusion(f32[10,10,10,384]{3,2,1,0:T(8,128)S(1)} %copy-done.3, f32[]{:T(128)} %bitcast.60, f32[10,384]{1,0:T(8,128)S(1)} %copy-done.18, f32[]{:T(128)} %bitcast.57, f32[10,384]{1,0:T(8,128)S(1)} %copy-done.22, f32[10,10,384]{2,1,0:T(8,128)} %broadcast_in_dim.546, f32[10,384]{1,0:T(8,128)S(1)} %copy-done.23, ...), kind=kOutput, calls=%fused_computation.67 | convolution fusion | flops 1811859456 | bytes 5103412 | tf_op jit(solution)/shard_map/abcj,ij->abci/dot_general | solution.py:192
  393.5 2.7 copy.48
  (236 shorter events, 54.6 us)
Async XLA Ops:
  11.6 31.0 %all-to-all-start.2 = ((f32[5,10,10,2,384]{4,2,1,0,3:T(8,128)}), f32[5,10,10,2,384]{4,2,1,0,3:T(8,128)S(1)}, u32[]{:S(2)}, u32[]{:S(2)}) async-start(f32[5,10,10,2,384]{4,2,1,0,3:T(8,128)} %copy.45), calls=%async_computation.2 | async-start | bytes 4915200 | tf_op jit(solution)/shard_map/all_to_all | solution.py:161
  18.9 29.9 %copy-start.31 = (s32[1,384]{1,0:T(1,128)S(1)}, s32[1,384]{1,0:T(1,128)}, u32[]{:S(2)}) copy-start(s32[1,384]{1,0:T(1,128)} %param.6) | copy-start | bytes 4612
  42.6 32.4 %all-to-all-start.1 = ((f32[5,10,10,2,384]{4,2,1,0,3:T(8,128)}), f32[5,10,10,2,384]{4,2,1,0,3:T(8,128)}, u32[]{:S(2)}, u32[]{:S(2)}) async-start(f32[5,10,10,2,384]{4,2,1,0,3:T(8,128)} %copy.42), calls=%async_computation.1 | async-start | bytes 4915200 | tf_op jit(solution)/shard_map/all_to_all | solution.py:160
  48.8 55.7 %copy-start.29 = (s32[384]{0:T(512)}, s32[384]{0:T(512)S(1)}, u32[]{:S(2)}) copy-start(s32[384]{0:T(512)S(1)} %reduce) | copy-start | bytes 4612
  53.0 138.5 %copy-start.25 = (pred[10]{0:T(512)(128)(4,1)}, pred[10]{0:T(512)(128)(4,1)S(1)}, u32[]{:S(2)}) copy-start(pred[10]{0:T(512)(128)(4,1)S(1)} %iota_compare_fusion.6) | copy-start | bytes 34
  75.0 21.7 %all-to-all-start = ((f32[2,5,10,10,1,384]{5,4,3,2,1,0:T(1,128)}), f32[2,5,10,10,1,384]{5,4,3,2,1,0:T(1,128)}, u32[]{:S(2)}, u32[]{:S(2)}) async-start(f32[2,5,10,10,1,384]{5,4,3,2,1,0:T(1,128)} %pad_maximum_fusion), calls=%async_computation | async-start | bytes 3072000 | tf_op jit(solution)/shard_map/all_to_all | solution.py:17
  81.2 110.3 %copy-start.27 = (pred[10]{0:T(512)(128)(4,1)}, pred[10]{0:T(512)(128)(4,1)S(1)}, u32[]{:S(2)}) copy-start(pred[10]{0:T(512)(128)(4,1)S(1)} %iota_compare_fusion.5) | copy-start | bytes 34
  90.8 7.5 %copy-start.7 = (f32[10,10,384,10]{2,3,1,0:T(8,128)S(1)}, f32[10,10,384,10]{2,3,1,0:T(8,128)}, u32[]{:S(2)}) copy-start(f32[10,10,384,10]{2,3,1,0:T(8,128)} %fusion.120) | copy-start | bytes 4608004
  107.4 15.4 %copy-start.2 = (f32[10,10,10,384]{3,2,1,0:T(8,128)}, f32[10,10,10,384]{3,2,1,0:T(8,128)S(1)}, u32[]{:S(2)}) copy-start(f32[10,10,10,384]{3,2,1,0:T(8,128)S(1)} %fusion.23) | copy-start | bytes 4608004
  134.1 33.8 %slice-start = ((s8[24576000]{0:T(1024)(128)(4,1)}), s8[4194304]{0:T(1024)(128)(4,1)S(1)}, s32[]{:S(2)}) async-start(s8[24576000]{0:T(1024)(128)(4,1)} %bitcast.192), calls=%async_computation.3 | async-start | bytes 8388608
  134.1 33.8 %slice-start.1 = ((s8[24576000]{0:T(1024)(128)(4,1)}), s8[4194304]{0:T(1024)(128)(4,1)S(1)}, s32[]{:S(2)}) async-start(s8[24576000]{0:T(1024)(128)(4,1)} %bitcast.192), calls=%async_computation.4 | async-start | bytes 8388608
  134.1 33.8 %slice-start.2 = ((s8[24576000]{0:T(1024)(128)(4,1)}), s8[4194304]{0:T(1024)(128)(4,1)S(1)}, s32[]{:S(2)}) async-start(s8[24576000]{0:T(1024)(128)(4,1)} %bitcast.192), calls=%async_computation.5 | async-start | bytes 8388608
  134.1 33.8 %slice-start.3 = ((s8[24576000]{0:T(1024)(128)(4,1)}), s8[4194304]{0:T(1024)(128)(4,1)S(1)}, s32[]{:S(2)}) async-start(s8[24576000]{0:T(1024)(128)(4,1)} %bitcast.192), calls=%async_computation.6 | async-start | bytes 8388608
  134.1 33.8 %slice-start.4 = ((s8[24576000]{0:T(1024)(128)(4,1)}), s8[4194304]{0:T(1024)(128)(4,1)S(1)}, s32[]{:S(2)}) async-start(s8[24576000]{0:T(1024)(128)(4,1)} %bitcast.192), calls=%async_computation.7 | async-start | bytes 8388608
  161.0 6.9 %slice-start.5 = ((s8[24576000]{0:T(1024)(128)(4,1)}), s8[3604480]{0:T(1024)(128)(4,1)S(1)}, s32[]{:S(2)}) async-start(s8[24576000]{0:T(1024)(128)(4,1)} %bitcast.192), calls=%async_computation.8 | async-start | bytes 7208960
  219.8 7.3 %copy-start.6 = (f32[1,10,10,6,8,8]{5,4,3,0,2,1:T(8,128)S(1)}, f32[1,10,10,6,8,8]{5,4,3,0,2,1:T(8,128)}, u32[]{:S(2)}) copy-start(f32[1,10,10,6,8,8]{5,4,3,0,2,1:T(8,128)} %get-tuple-element.50) | copy-start | bytes 460804
  228.3 7.0 %copy-start.4 = (f32[10,1,10,6,8,8]{5,4,3,2,1,0:T(8,128)S(1)}, f32[10,1,10,6,8,8]{5,4,3,2,1,0:T(8,128)}, u32[]{:S(2)}) copy-start(f32[10,1,10,6,8,8]{5,4,3,2,1,0:T(8,128)} %get-tuple-element.55) | copy-start | bytes 460804
  243.1 31.7 %copy-start.9 = (f32[1,10,10,1,8,8]{5,4,3,2,1,0:T(8,128)S(1)}, f32[1,10,10,1,8,8]{5,4,3,2,1,0:T(8,128)}, u32[]{:S(2)}) copy-start(f32[1,10,10,1,8,8]{5,4,3,2,1,0:T(8,128)} %get-tuple-element.30) | copy-start | bytes 76804
  243.1 32.5 %collective-permute-start = (f32[1]{0:T(128)}, f32[1]{0:T(128)}, u32[]{:S(2)}, u32[]{:S(2)}) collective-permute-start(f32[1]{0:T(128)} %bitcast.38), channel_id=1, source_target_pairs={{0,21},{1,22},{2,23},{3,24},{4,25},{5,26},{6,27},{7,28},{8,29},{9,... | collective-permute-start | bytes 20 | tf_op jit(solution)/shard_map/ppermute | solution.py:24
  253.0 24.5 %collective-permute-start.25 = (f32[1]{0:T(128)}, f32[1]{0:T(128)}, u32[]{:S(2)}, u32[]{:S(2)}) collective-permute-start(f32[1]{0:T(128)} %bitcast.59), channel_id=1, source_target_pairs={{21,0},{22,1},{23,2},{24,3},{25,4},{26,5},{27,6},{28,7},{29,8},{30... | collective-permute-start | bytes 20 | tf_op jit(solution)/shard_map/ppermute | solution.py:24
  254.3 30.2 %collective-permute-start.19 = (f32[1]{0:T(128)}, f32[1]{0:T(128)}, u32[]{:S(2)}, u32[]{:S(2)}) collective-permute-start(f32[1]{0:T(128)} %bitcast.53), channel_id=1, source_target_pairs={{13,0},{14,1},{15,2},{16,3},{17,4},{18,5},{19,6},{20,7},{21,8},{22... | collective-permute-start | bytes 20 | tf_op jit(solution)/shard_map/ppermute | solution.py:24
  255.6 32.5 %collective-permute-start.17 = (f32[1]{0:T(128)}, f32[1]{0:T(128)}, u32[]{:S(2)}, u32[]{:S(2)}) collective-permute-start(f32[1]{0:T(128)} %bitcast.50), channel_id=1, source_target_pairs={{11,0},{12,1},{13,2},{14,3},{15,4},{16,5},{17,6},{18,7},{19,8},{20... | collective-permute-start | bytes 20 | tf_op jit(solution)/shard_map/ppermute | solution.py:24
  256.9 33.8 %collective-permute-start.8 = (f32[1]{0:T(128)}, f32[1]{0:T(128)}, u32[]{:S(2)}, u32[]{:S(2)}) collective-permute-start(f32[1]{0:T(128)} %bitcast.47), channel_id=1, source_target_pairs={{0,11},{1,12},{2,13},{3,14},{4,15},{5,16},{6,17},{7,18},{8,19},{9,... | collective-permute-start | bytes 20 | tf_op jit(solution)/shard_map/ppermute | solution.py:24
  275.6 19.4 %collective-permute-start.23 = (f32[1]{0:T(128)}, f32[1]{0:T(128)}, u32[]{:S(2)}, u32[]{:S(2)}) collective-permute-start(f32[1]{0:T(128)} %bitcast.56), channel_id=1, source_target_pairs={{19,0},{20,1},{21,2},{22,3},{23,4},{24,5},{25,6},{26,7},{27,8},{28... | collective-permute-start | bytes 20 | tf_op jit(solution)/shard_map/ppermute | solution.py:24
  277.5 20.0 %collective-permute-start.6 = (f32[1]{0:T(128)}, f32[1]{0:T(128)}, u32[]{:S(2)}, u32[]{:S(2)}) collective-permute-start(f32[1]{0:T(128)} %bitcast.44), channel_id=1, source_target_pairs={{0,13},{1,14},{2,15},{3,16},{4,17},{5,18},{6,19},{7,20},{8,21},{9,... | collective-permute-start | bytes 20 | tf_op jit(solution)/shard_map/ppermute | solution.py:24
  284.5 18.1 %collective-permute-start.2 = (f32[1]{0:T(128)}, f32[1]{0:T(128)}, u32[]{:S(2)}, u32[]{:S(2)}) collective-permute-start(f32[1]{0:T(128)} %bitcast.41), channel_id=1, source_target_pairs={{0,19},{1,20},{2,21},{3,22},{4,23},{5,24},{6,25},{7,26},{8,27},{9,... | collective-permute-start | bytes 20 | tf_op jit(solution)/shard_map/ppermute | solution.py:24
  288.1 16.8 %collective-permute-start.11 = (f32[60]{0:T(128)S(1)}, f32[60]{0:T(128)S(1)}, u32[]{:S(2)}, u32[]{:S(2)}) collective-permute-start(f32[60]{0:T(128)S(1)} %reshape.232), channel_id=1, source_target_pairs={{0,3},{1,4},{2,5},{3,6},{4,7},{5,8},{6,9},{7,10},{8,11},{9,12},{10... | collective-permute-start | bytes 728 | tf_op jit(solution)/shard_map/ppermute | solution.py:24
  290.7 15.6 %collective-permute-start.14 = (f32[60]{0:T(128)S(1)}, f32[60]{0:T(128)S(1)}, u32[]{:S(2)}, u32[]{:S(2)}) collective-permute-start(f32[60]{0:T(128)S(1)} %reshape.235), channel_id=1, source_target_pairs={{3,0},{4,1},{5,2},{6,3},{7,4},{8,5},{9,6},{10,7},{11,8},{12,9},{13... | collective-permute-start | bytes 728 | tf_op jit(solution)/shard_map/ppermute | solution.py:24
  295.0 12.6 %collective-permute-start.16 = (f32[60]{0:T(128)S(1)}, f32[60]{0:T(128)S(1)}, u32[]{:S(2)}, u32[]{:S(2)}) collective-permute-start(f32[60]{0:T(128)S(1)} %reshape.237), channel_id=1, source_target_pairs={{5,0},{6,1},{7,2},{8,3},{9,4},{10,5},{11,6},{12,7},{13,8},{14,9},{... | collective-permute-start | bytes 728 | tf_op jit(solution)/shard_map/ppermute | solution.py:24
  297.5 18.2 %collective-permute-start.9 = (f32[60]{0:T(128)S(1)}, f32[60]{0:T(128)S(1)}, u32[]{:S(2)}, u32[]{:S(2)}) collective-permute-start(f32[60]{0:T(128)S(1)} %reshape.230), channel_id=1, source_target_pairs={{0,5},{1,6},{2,7},{3,8},{4,9},{5,10},{6,11},{7,12},{8,13},{9,14},{... | collective-permute-start | bytes 728 | tf_op jit(solution)/shard_map/ppermute | solution.py:24
  302.6 18.0 %collective-permute-start.5 = (f32[80]{0:T(128)S(1)}, f32[80]{0:T(128)S(1)}, u32[]{:S(2)}, u32[]{:S(2)}) collective-permute-start(f32[80]{0:T(128)S(1)} %reshape.226), channel_id=1, source_target_pairs={{0,15},{1,16},{2,17},{3,18},{4,19},{5,20},{6,21},{7,22},{8,23},{9,... | collective-permute-start | bytes 968 | tf_op jit(solution)/shard_map/ppermute | solution.py:24
  304.9 17.0 %collective-permute-start.20 = (f32[80]{0:T(128)S(1)}, f32[80]{0:T(128)S(1)}, u32[]{:S(2)}, u32[]{:S(2)}) collective-permute-start(f32[80]{0:T(128)S(1)} %reshape.241), channel_id=1, source_target_pairs={{15,0},{16,1},{17,2},{18,3},{19,4},{20,5},{21,6},{22,7},{23,8},{24... | collective-permute-start | bytes 968 | tf_op jit(solution)/shard_map/ppermute | solution.py:24
  306.3 17.0 %collective-permute-start.22 = (f32[80]{0:T(128)S(1)}, f32[80]{0:T(128)S(1)}, u32[]{:S(2)}, u32[]{:S(2)}) collective-permute-start(f32[80]{0:T(128)S(1)} %reshape.243), channel_id=1, source_target_pairs={{17,0},{18,1},{19,2},{20,3},{21,4},{22,5},{23,6},{24,7},{25,8},{26... | collective-permute-start | bytes 968 | tf_op jit(solution)/shard_map/ppermute | solution.py:24
  307.6 22.4 %collective-permute-start.3 = (f32[80]{0:T(128)S(1)}, f32[80]{0:T(128)S(1)}, u32[]{:S(2)}, u32[]{:S(2)}) collective-permute-start(f32[80]{0:T(128)S(1)} %reshape.224), channel_id=1, source_target_pairs={{0,17},{1,18},{2,19},{3,20},{4,21},{5,22},{6,23},{7,24},{8,25},{9,... | collective-permute-start | bytes 968 | tf_op jit(solution)/shard_map/ppermute | solution.py:24
  315.7 16.2 %collective-permute-start.7 = (f32[80]{0:T(128)S(1)}, f32[80]{0:T(128)S(1)}, u32[]{:S(2)}, u32[]{:S(2)}) collective-permute-start(f32[80]{0:T(128)S(1)} %reshape.228), channel_id=1, source_target_pairs={{0,12},{1,13},{2,14},{3,15},{4,16},{5,17},{6,18},{7,19},{8,20},{9,... | collective-permute-start | bytes 968 | tf_op jit(solution)/shard_map/ppermute | solution.py:24
  320.6 16.8 %collective-permute-start.18 = (f32[80]{0:T(128)S(1)}, f32[80]{0:T(128)S(1)}, u32[]{:S(2)}, u32[]{:S(2)}) collective-permute-start(f32[80]{0:T(128)S(1)} %reshape.239), channel_id=1, source_target_pairs={{12,0},{13,1},{14,2},{15,3},{16,4},{17,5},{18,6},{19,7},{20,8},{21... | collective-permute-start | bytes 968 | tf_op jit(solution)/shard_map/ppermute | solution.py:24
  322.0 17.4 %collective-permute-start.24 = (f32[80]{0:T(128)S(1)}, f32[80]{0:T(128)S(1)}, u32[]{:S(2)}, u32[]{:S(2)}) collective-permute-start(f32[80]{0:T(128)S(1)} %reshape.245), channel_id=1, source_target_pairs={{20,0},{21,1},{22,2},{23,3},{24,4},{25,5},{26,6},{27,7},{28,8},{29... | collective-permute-start | bytes 968 | tf_op jit(solution)/shard_map/ppermute | solution.py:24
  323.3 20.4 %collective-permute-start.1 = (f32[80]{0:T(128)S(1)}, f32[80]{0:T(128)S(1)}, u32[]{:S(2)}, u32[]{:S(2)}) collective-permute-start(f32[80]{0:T(128)S(1)} %reshape.222), channel_id=1, source_target_pairs={{0,20},{1,21},{2,22},{3,23},{4,24},{5,25},{6,26},{7,27},{8,28},{9,... | collective-permute-start | bytes 968 | tf_op jit(solution)/shard_map/ppermute | solution.py:24
  330.0 22.1 %collective-permute-start.13 = (f32[4800]{0:T(1024)S(1)}, f32[4800]{0:T(1024)S(1)}, u32[]{:S(2)}, u32[]{:S(2)}) collective-permute-start(f32[4800]{0:T(1024)S(1)} %reshape.234), channel_id=1, source_target_pairs={{1,0},{2,1},{3,2},{4,3},{5,4},{6,5},{7,6},{8,7},{9,8},{10,9},{11,1... | collective-permute-start | bytes 57608 | tf_op jit(solution)/shard_map/ppermute | solution.py:24
  331.9 25.8 %collective-permute-start.12 = (f32[4800]{0:T(1024)S(1)}, f32[4800]{0:T(1024)S(1)}, u32[]{:S(2)}, u32[]{:S(2)}) collective-permute-start(f32[4800]{0:T(1024)S(1)} %reshape.233), channel_id=1, source_target_pairs={{0,1},{1,2},{2,3},{3,4},{4,5},{5,6},{6,7},{7,8},{8,9},{9,10},{10,1... | collective-permute-start | bytes 57608 | tf_op jit(solution)/shard_map/ppermute | solution.py:24
  337.4 20.4 %collective-permute-start.15 = (f32[4800]{0:T(1024)S(1)}, f32[4800]{0:T(1024)S(1)}, u32[]{:S(2)}, u32[]{:S(2)}) collective-permute-start(f32[4800]{0:T(1024)S(1)} %reshape.236), channel_id=1, source_target_pairs={{4,0},{5,1},{6,2},{7,3},{8,4},{9,5},{10,6},{11,7},{12,8},{13,9},{1... | collective-permute-start | bytes 57608 | tf_op jit(solution)/shard_map/ppermute | solution.py:24
  339.4 18.4 %collective-permute-start.10 = (f32[4800]{0:T(1024)S(1)}, f32[4800]{0:T(1024)S(1)}, u32[]{:S(2)}, u32[]{:S(2)}) collective-permute-start(f32[4800]{0:T(1024)S(1)} %reshape.231), channel_id=1, source_target_pairs={{0,4},{1,5},{2,6},{3,7},{4,8},{5,9},{6,10},{7,11},{8,12},{9,13},{1... | collective-permute-start | bytes 57608 | tf_op jit(solution)/shard_map/ppermute | solution.py:24
  343.7 28.2 %collective-permute-start.21 = (f32[6400]{0:T(1024)}, f32[6400]{0:T(1024)S(1)}, u32[]{:S(2)}, u32[]{:S(2)}) collective-permute-start(f32[6400]{0:T(1024)} %reshape.242), channel_id=1, source_target_pairs={{16,0},{17,1},{18,2},{19,3},{20,4},{21,5},{22,6},{23,7},{24,8},{25... | collective-permute-start | bytes 76808 | tf_op jit(solution)/shard_map/ppermute | solution.py:24
  352.1 19.5 %collective-permute-start.4 = (f32[6400]{0:T(1024)}, f32[6400]{0:T(1024)}, u32[]{:S(2)}, u32[]{:S(2)}) collective-permute-start(f32[6400]{0:T(1024)} %reshape.225), channel_id=1, source_target_pairs={{0,16},{1,17},{2,18},{3,19},{4,20},{5,21},{6,22},{7,23},{8,24},{9,... | collective-permute-start | bytes 76808 | tf_op jit(solution)/shard_map/ppermute | solution.py:24
  374.2 5.5 %copy-start.3 = (f32[10,10,10,384]{3,2,1,0:T(8,128)S(1)}, f32[10,10,10,384]{3,2,1,0:T(8,128)}, u32[]{:S(2)}) copy-start(f32[10,10,10,384]{3,2,1,0:T(8,128)} %copy-done.2) | copy-start | bytes 4608004
  374.2 5.5 %copy-start.10 = (f32[10,10,384]{2,1,0:T(8,128)S(1)}, f32[10,10,384]{2,1,0:T(8,128)}, u32[]{:S(2)}) copy-start(f32[10,10,384]{2,1,0:T(8,128)} %broadcast_in_dim.442) | copy-start | bytes 460804
  374.2 5.6 %copy-start.13 = (f32[10,384]{1,0:T(8,128)S(1)}, f32[10,384]{1,0:T(8,128)}, u32[]{:S(2)}) copy-start(f32[10,384]{1,0:T(8,128)} %broadcast_in_dim.501) | copy-start | bytes 46084
  374.2 5.6 %copy-start.14 = (f32[10,384]{1,0:T(8,128)S(1)}, f32[10,384]{1,0:T(8,128)}, u32[]{:S(2)}) copy-start(f32[10,384]{1,0:T(8,128)} %broadcast_in_dim.530) | copy-start | bytes 46084
  374.2 5.6 %copy-start.15 = (f32[10,384]{1,0:T(8,128)S(1)}, f32[10,384]{1,0:T(8,128)}, u32[]{:S(2)}) copy-start(f32[10,384]{1,0:T(8,128)} %broadcast_in_dim.522) | copy-start | bytes 46084
  374.2 5.6 %copy-start.16 = (f32[10,384]{1,0:T(8,128)S(1)}, f32[10,384]{1,0:T(8,128)}, u32[]{:S(2)}) copy-start(f32[10,384]{1,0:T(8,128)} %broadcast_in_dim.510) | copy-start | bytes 46084
  374.3 5.6 %copy-start.17 = (f32[10,384]{1,0:T(8,128)S(1)}, f32[10,384]{1,0:T(8,128)}, u32[]{:S(2)}) copy-start(f32[10,384]{1,0:T(8,128)} %broadcast_in_dim.473) | copy-start | bytes 46084
  374.3 5.6 %copy-start.18 = (f32[10,384]{1,0:T(8,128)S(1)}, f32[10,384]{1,0:T(8,128)}, u32[]{:S(2)}) copy-start(f32[10,384]{1,0:T(8,128)} %broadcast_in_dim.556) | copy-start | bytes 46084
  374.3 5.6 %copy-start.19 = (f32[10,384]{1,0:T(8,128)S(1)}, f32[10,384]{1,0:T(8,128)}, u32[]{:S(2)}) copy-start(f32[10,384]{1,0:T(8,128)} %broadcast_in_dim.536) | copy-start | bytes 46084
  374.3 5.6 %copy-start.26 = (pred[10]{0:T(512)(128)(4,1)S(1)}, pred[10]{0:T(512)(128)(4,1)}, u32[]{:S(2)}) copy-start(pred[10]{0:T(512)(128)(4,1)} %copy-done.25) | copy-start | bytes 34
  374.3 5.6 %copy-start.28 = (pred[10]{0:T(512)(128)(4,1)S(1)}, pred[10]{0:T(512)(128)(4,1)}, u32[]{:S(2)}) copy-start(pred[10]{0:T(512)(128)(4,1)} %copy-done.27) | copy-start | bytes 34
  374.3 5.6 %copy-start.30 = (s32[384]{0:T(512)S(1)}, s32[384]{0:T(512)}, u32[]{:S(2)}) copy-start(s32[384]{0:T(512)} %copy-done.29) | copy-start | bytes 4612
  374.3 5.6 %copy-start.32 = (pred[384]{0:T(512)(128)(4,1)S(1)}, pred[384]{0:T(512)(128)(4,1)}, u32[]{:S(2)}) copy-start(pred[384]{0:T(512)(128)(4,1)} %iota.888) | copy-start | bytes 1156
  374.3 5.6 %copy-start.33 = (pred[384]{0:T(512)(128)(4,1)S(1)}, pred[384]{0:T(512)(128)(4,1)}, u32[]{:S(2)}) copy-start(pred[384]{0:T(512)(128)(4,1)} %iota.868) | copy-start | bytes 1156
  374.3 5.6 %copy-start.34 = (pred[384]{0:T(512)(128)(4,1)S(1)}, pred[384]{0:T(512)(128)(4,1)}, u32[]{:S(2)}) copy-start(pred[384]{0:T(512)(128)(4,1)} %iota.884) | copy-start | bytes 1156
  375.9 4.0 %copy-start.23 = (f32[10,384]{1,0:T(8,128)S(1)}, f32[10,384]{1,0:T(8,128)}, u32[]{:S(2)}) copy-start(f32[10,384]{1,0:T(8,128)} %broadcast_in_dim.542) | copy-start | bytes 46084
  375.9 4.0 %copy-start.24 = (f32[10,384]{1,0:T(8,128)S(1)}, f32[10,384]{1,0:T(8,128)}, u32[]{:S(2)}) copy-start(f32[10,384]{1,0:T(8,128)} %broadcast_in_dim.488) | copy-start | bytes 46084
  376.0 4.0 %copy-start.35 = (pred[384]{0:T(512)(128)(4,1)S(1)}, pred[384]{0:T(512)(128)(4,1)}, u32[]{:S(2)}) copy-start(pred[384]{0:T(512)(128)(4,1)} %iota.881) | copy-start | bytes 1156
  376.0 4.0 %copy-start.36 = (pred[384]{0:T(512)(128)(4,1)S(1)}, pred[384]{0:T(512)(128)(4,1)}, u32[]{:S(2)}) copy-start(pred[384]{0:T(512)(128)(4,1)} %iota.875) | copy-start | bytes 1156
  376.0 4.0 %copy-start.37 = (pred[384]{0:T(512)(128)(4,1)S(1)}, pred[384]{0:T(512)(128)(4,1)}, u32[]{:S(2)}) copy-start(pred[384]{0:T(512)(128)(4,1)} %iota.872) | copy-start | bytes 1156
  (11 other events, 32.9 us)
